TPU v7x, 64 devices: a 2x2x8 block of a 4x4x8 slice. The times are simulated.
64 devices in a mesh: req: 4 (over x, y), cp: 16 (over z, core).
Axes of the slice: x: 2, y: 2, z: 8, core: 2. Of those that a mesh axis runs over, the one named last changes fastest.
The devices are a block of a 4x4x8 slice.
Arguments:
- x: bfloat16 [16384, 2048], P(('req', 'cp')), parts along dimension 0
- pos: int32 [16384], P(('req', 'cp')), parts along dimension 0
- g1: bfloat16 [2, 2048], replicated
- g2: bfloat16 [2, 2048], replicated
- wq: bfloat16 [2, 2048, 2048], replicated
- wk: bfloat16 [2, 2048, 2048], replicated
- wv: bfloat16 [2, 2048, 2048], replicated
- wo: bfloat16 [2, 2048, 2048], replicated
- w1: bfloat16 [2, 2048, 5504], replicated
- w3: bfloat16 [2, 2048, 5504], replicated
- w2: bfloat16 [2, 5504, 2048], replicated
Outputs:
- output 1: bfloat16 [16384, 2048], P(('req', 'cp')), parts along dimension 0
- output 2: bfloat16 [2, 16384, 16, 128], P(None, 'req', 'cp'), parts along dimension 1
- output 3: bfloat16 [2, 16384, 16, 128], P(None, 'req', 'cp'), parts along dimension 1
There are 4 independent parts. A program takes and returns all parts, laid end to end along the dimension named above; an argument that names none is the same for every part.
All inputs are finite; a program needn't handle non-finite values.
Results may differ from a plain program's by a relative error of at most 0.0181633.
Values are sent between devices in bfloat16 or wider.
A program may use at most 768 MiB of HBM per device.

v0:
```python
import jax
import jax.numpy as jnp
from jax import lax
from jax.sharding import PartitionSpec as P

HEAD = 128
F32 = jnp.float32
BF16 = jnp.bfloat16


def _norm(x, g):
    x32 = x.astype(F32)
    r = lax.rsqrt(jnp.mean(x32 * x32, axis=-1, keepdims=True) + 1e-5)
    return (x32 * r * g.astype(F32)).astype(BF16)


def _angles(pos):
    half = HEAD // 2
    inv = 1.0 / (10000.0 ** (jnp.arange(half, dtype=F32) * (2.0 / HEAD)))
    ang = pos.astype(F32)[..., None] * inv
    return jnp.cos(ang)[..., None, :], jnp.sin(ang)[..., None, :]


def _rope(t, c, sn):
    half = HEAD // 2
    t1, t2 = t[..., :half], t[..., half:]
    return jnp.concatenate([t1 * c - t2 * sn, t2 * c + t1 * sn], axis=-1)


def _attention(q, kg, vg, mask):
    def one(a):
        qh, kh, vh = a
        sc = jnp.einsum('qd,kd->qk', qh, kh, preferred_element_type=F32) * HEAD ** -0.5
        p = jax.nn.softmax(jnp.where(mask, sc, -jnp.inf), axis=-1).astype(BF16)
        return jnp.dot(p, vh, preferred_element_type=F32).astype(BF16)

    o = lax.map(one, (q.transpose(1, 0, 2), kg.transpose(1, 0, 2), vg.transpose(1, 0, 2)))
    return o.transpose(1, 0, 2).reshape(q.shape[0], -1)


def _natural(a, ncp):
    n, seq = a.shape[0], a.shape[1]
    a = a.reshape((n, ncp, 2, seq // (2 * ncp)) + a.shape[2:])
    a = jnp.concatenate([a[:, :, 0], a[:, ::-1, 1]], axis=1)
    return a.reshape((n, seq) + a.shape[3:])


def solution(mesh):
    ncp = mesh.shape['cp']
    act = P(('req', 'cp'), None)
    cache = P(None, 'req', 'cp', None)

    def body(x, pos, g1, g2, wq, wk, wv, wo, w1, w3, w2):
        s_dev = x.shape[0]
        nh = wq.shape[2] // HEAD
        pos_all = lax.all_gather(pos, 'cp', tiled=True)
        mask = pos_all[None, :] <= pos[:, None]
        c, sn = _angles(pos)
        kl, vl = [], []
        for l in range(wq.shape[0]):
            h = _norm(x, g1[l])
            q = _rope(jnp.dot(h, wq[l], preferred_element_type=F32).reshape(s_dev, nh, HEAD), c, sn).astype(BF16)
            k = _rope(jnp.dot(h, wk[l], preferred_element_type=F32).reshape(s_dev, nh, HEAD), c, sn).astype(BF16)
            v = jnp.dot(h, wv[l], preferred_element_type=F32).astype(BF16).reshape(s_dev, nh, HEAD)
            kg = lax.all_gather(k, 'cp', tiled=True)
            vg = lax.all_gather(v, 'cp', tiled=True)
            o = _attention(q, kg, vg, mask)
            x = (x.astype(F32) + jnp.dot(o, wo[l], preferred_element_type=F32)).astype(BF16)
            h2 = _norm(x, g2[l])
            u = (jax.nn.silu(jnp.dot(h2, w1[l], preferred_element_type=F32))
                 * jnp.dot(h2, w3[l], preferred_element_type=F32)).astype(BF16)
            x = (x.astype(F32) + jnp.dot(u, w2[l], preferred_element_type=F32)).astype(BF16)
            kl.append(k)
            vl.append(v)
        kc = _natural(lax.all_to_all(jnp.stack(kl), 'cp', 2, 1, tiled=True), ncp)
        vc = _natural(lax.all_to_all(jnp.stack(vl), 'cp', 2, 1, tiled=True), ncp)
        return x, kc, vc

    return jax.shard_map(body, mesh=mesh, in_specs=(act, P(('req', 'cp'))) + (P(),) * 9,
                         out_specs=(act, cache, cache), check_vma=False)
```

profile of v0, /device:TPU:21, one launch (start us, length us, event | category | flops | bytes accessed | tf_op | source)
XLA Modules:
  0.0 814.1 jit_solution(3100207017543313121)
XLA Ops:
  10.2 11.9 %slice_bitcast_fusion = (bf16[2048,2048]{0,1:T(8,128)(2,1)}, bf16[2048,2048]{0,1:T(8,128)(2,1)}) fusion(bf16[2,2048,2048]{2,1,0:T(8,128)(2,1)} %param.20), kind=kLoop, calls=%fused_computation.64 | loop fusion | bytes 33554432 | tf_op jit(solution)/shard_map/dot_general | solution.py:63
  22.1 12.4 %copy.64 = bf16[2048,2048]{1,0:T(8,128)(2,1)} copy(bf16[2048,2048]{0,1:T(8,128)(2,1)} %get-tuple-element.203) | data formatting | bytes 16777216 | tf_op jit(solution)/shard_map/dot_general | solution.py:63
  34.4 11.8 %slice_bitcast_fusion.3 = (bf16[2048,2048]{0,1:T(8,128)(2,1)}, bf16[2048,2048]{0,1:T(8,128)(2,1)}) fusion(bf16[2,2048,2048]{2,1,0:T(8,128)(2,1)} %param.19), kind=kLoop, calls=%fused_computation.69 | loop fusion | bytes 33554432 | tf_op jit(solution)/shard_map/dot_general | solution.py:62
  46.3 12.4 %copy.63 = bf16[2048,2048]{1,0:T(8,128)(2,1)} copy(bf16[2048,2048]{0,1:T(8,128)(2,1)} %get-tuple-element.204) | data formatting | bytes 16777216 | tf_op jit(solution)/shard_map/dot_general | solution.py:62
  58.7 6.0 fusion.114
  64.7 2.5 fusion.116
  70.1 6.1 fusion.92
  77.6 22.8 %all-gather = s32[16,1,256]{2,1,0:T(1,128)S(1)} all-gather(s32[1,1,256]{2,1,0:T(1,128)S(1)} %bitcast.237), channel_id=1, replica_groups=mesh['req'=4,'cp'=16] {'cp'}, dimensions={0}, use_global_device_ids=true | all-gather | bytes 17408 | tf_op jit(solution)/shard_map/all_gather | solution.py:56
  103.2 70.0 %all-gather.6.cloned.1.call-done = bf16[4096,16,128]{0,2,1:T(8,128)(2,1)} async-done(((bf16[256,16,128]{0,2,1:T(8,128)(2,1)}), bf16[4096,16,128]{0,2,1:T(8,128)(2,1)}) %all-gather.6.cloned.1.call-update) | async-done | bytes 16777232 | tf_op jit(solution)/shard_map/all_gather | solution.py:65
  173.2 92.0 %all-gather.8.cloned.1.call-done = bf16[4096,16,128]{2,0,1:T(8,128)(2,1)} async-done(((bf16[256,16,128]{2,0,1:T(8,128)(2,1)}), bf16[4096,16,128]{2,0,1:T(8,128)(2,1)}) %all-gather.8.cloned.1.call-update) | async-done | bytes 16777232 | tf_op jit(solution)/shard_map/all_gather | solution.py:66
  266.3 94.6 %while.22 = (s32[]{:T(128)}, bf16[16,256,128]{1,2,0:T(8,128)(2,1)}, bf16[16,256,128]{1,2,0:T(8,128)(2,1)}, bf16[16,4096,128]{1,2,0:T(8,128)(2,1)}, bf16[16,4096,...) while((s32[]{:T(128)}, bf16[16,256,128]{1,2,0:T(8,128)(2,1)}, ...), condition=%wide.region_4.5_spmd.clone, body=%wide.region_1.4_spmd.clone.sunk | while | flops 546340352 | bytes 15097941 | solution.py:37
  298.9 2.2 fusion.163
  304.8 2.2 fusion.163
  360.9 6.4 fusion.101
  368.3 12.4 %fusion.40 = f32[256,5504]{1,0:T(8,128)} fusion(bf16[2,2048,5504]{2,1,0:T(8,128)(2,1)} %param.23, bf16[256,2048]{1,0:T(8,128)(2,1)S(1)} %get-tuple-element.229, f32[2048]{0:T(1024)S(1)} %bitcast.247, f32[256]{0:T(256)S(1)} %add_rsqrt_fusion.2), kind=kOutput, calls=%fused_computation.46 | convolution fusion | flops 5773459456 | bytes 29238272 | tf_op jit(solution)/shard_map/dot_general | solution.py:70
  380.7 25.9 %fusion.104 = (f32[256]{0:T(256)S(1)}, bf16[256,2048]{1,0:T(8,128)(2,1)}) fusion(bf16[2,5504,2048]{2,1,0:T(8,128)(2,1)} %param.25, bf16[2,2048,5504]{2,1,0:T(8,128)(2,1)} %param.24, f32[256,5504]{1,0:T(8,128)} %fusion.40, bf16[256,2048]{1,0:T(8,128)(2,1)} %copy-done.13, f32[2048]{0:T(1024)S(1)} %bitcast.248, f32[256]{0:T(256)S(1)} %add_rsqrt_fusion.2), kind=kOutput, calls=%fused_computation.98 | convolution fusion | flops 11556421632 | bytes 53880832 | tf_op jit(solution)/shard_map/dot_general | solution.py:72
  406.7 6.1 fusion.95
  415.1 12.5 %copy.69 = bf16[2048,2048]{1,0:T(8,128)(2,1)} copy(bf16[2048,2048]{0,1:T(8,128)(2,1)} %get-tuple-element.205) | data formatting | bytes 16777216 | tf_op jit(solution)/shard_map/dot_general | solution.py:62
  427.7 12.1 %copy.70 = bf16[2048,2048]{1,0:T(8,128)(2,1)} copy(bf16[2048,2048]{0,1:T(8,128)(2,1)} %get-tuple-element.202) | data formatting | bytes 16777216 | tf_op jit(solution)/shard_map/dot_general | solution.py:63
  439.8 6.3 fusion.112
  446.1 2.5 fusion.110
  456.0 4.7 all-to-all-start.1
  463.7 67.3 %all-to-all-done.1 = bf16[2,256,16,128]{3,1,0,2:T(8,128)(2,1)S(1)} async-done(((bf16[2,256,16,128]{3,1,0,2:T(8,128)(2,1)}), bf16[2,256,16,128]{3,1,0,2:T(8,128)(2,1)S(1)}, u32[]{:S(2)}, u32[]{:S(2)}) %all-to-all-start.1) | async-done | bytes 2097184 | tf_op jit(solution)/shard_map/all_to_all | solution.py:76
  531.1 6.9 all-to-all-start
  541.1 56.6 %all-to-all-done = bf16[2,256,16,128]{1,3,0,2:T(8,128)(2,1)} async-done(((bf16[2,256,16,128]{1,3,0,2:T(8,128)(2,1)}), bf16[2,256,16,128]{1,3,0,2:T(8,128)(2,1)}, u32[]{:S(2)}, u32[]{:S(2)}) %all-to-all-start) | async-done | bytes 2097184 | tf_op jit(solution)/shard_map/all_to_all | solution.py:75
  597.7 3.0 copy.76
  602.4 79.7 %all-gather.10.cloned.1.call-done = bf16[4096,16,128]{0,2,1:T(8,128)(2,1)} async-done(((bf16[256,16,128]{0,2,1:T(8,128)(2,1)}), bf16[4096,16,128]{0,2,1:T(8,128)(2,1)}) %all-gather.10.cloned.1.call-update) | async-done | bytes 16777232 | tf_op jit(solution)/shard_map/all_gather | solution.py:65
  682.3 84.9 %while.23 = (s32[]{:T(128)}, bf16[16,256,128]{1,2,0:T(8,128)(2,1)S(1)}, bf16[16,256,128]{1,2,0:T(8,128)(2,1)}, bf16[16,4096,128]{1,2,0:T(8,128)(2,1)}, bf16[16,4...) while((s32[]{:T(128)}, bf16[16,256,128]{1,2,0:T(8,128)(2,1)S(1)}, ...), condition=%wide.region_10.11_spmd.clone, body=%wide.region_7.10_spmd.clone.sunk | while | flops 546340352 | bytes 15097433 | solution.py:37
  685.2 2.2 fusion.167
  767.2 6.1 fusion.107
  773.3 12.4 %fusion.34 = f32[256,5504]{1,0:T(8,128)} fusion(bf16[2,2048,5504]{2,1,0:T(8,128)(2,1)} %param.23, bf16[256,2048]{1,0:T(8,128)(2,1)S(1)} %get-tuple-element.233, f32[2048]{0:T(1024)S(1)} %bitcast.242, f32[256]{0:T(256)S(1)} %add_rsqrt_fusion), kind=kOutput, calls=%fused_computation.40 | convolution fusion | flops 5773459456 | bytes 29238272 | tf_op jit(solution)/shard_map/dot_general | solution.py:70
  785.6 21.4 %fusion.83 = bf16[256,2048]{1,0:T(8,128)(2,1)} fusion(bf16[2,5504,2048]{2,1,0:T(8,128)(2,1)} %param.25, bf16[256,2048]{1,0:T(8,128)(2,1)S(1)} %get-tuple-element.233, bf16[2,2048,5504]{2,1,0:T(8,128)(2,1)} %param.24, f32[256,5504]{1,0:T(8,128)} %fusion.34, f32[2048]{0:T(1024)S(1)} %bitcast.243, f32[256]{0:T(256)S(1)} %add_rsqrt_fusion), kind=kOutput, calls=%fused_computation.87 | convolution fusion | flops 11554848768 | bytes 53879808 | tf_op jit(solution)/shard_map/dot_general | solution.py:72
  (228 shorter events, 201.4 us)
Async XLA Ops:
  7.2 166.0 %all-gather.6.cloned.1.call-start = ((), (), s32[]{:S(2)}) async-start(), calls=%async_computation.2 | async-start | bytes 17825792 | tf_op jit(solution)/shard_map/all_gather | solution.py:65
  46.3 12.4 %copy-start.8 = (bf16[256,2048]{1,0:T(8,128)(2,1)S(1)}, bf16[256,2048]{1,0:T(8,128)(2,1)}, u32[]{:S(2)}) copy-start(bf16[256,2048]{1,0:T(8,128)(2,1)} %param.15) | copy-start | bytes 3145732
  58.7 6.0 copy-start.1
  64.7 2.5 copy-start.7
  70.1 195.2 %all-gather.8.cloned.1.call-start = ((), (), s32[]{:S(2)}) async-start(), calls=%async_computation.3 | async-start | bytes 17825792 | tf_op jit(solution)/shard_map/all_gather | solution.py:66
  76.2 26.3 %copy-start.9 = (bf16[2,2048]{1,0:T(2,128)(2,1)S(1)}, bf16[2,2048]{1,0:T(2,128)(2,1)}, u32[]{:S(2)}) copy-start(bf16[2,2048]{1,0:T(2,128)(2,1)} %param.18) | copy-start | bytes 24580
  77.6 524.9 %all-gather.12.cloned.1.call-start = ((), (), s32[]{:S(2)}) async-start(), calls=%async_computation.5 | async-start | bytes 17825792 | tf_op jit(solution)/shard_map/all_gather | solution.py:66
  367.3 1.0 copy-start.13
  380.7 25.9 %copy-start.11 = (f32[1,2048]{1,0:T(1,128)S(1)}, f32[1,2048]{1,0:T(1,128)}, u32[]{:S(2)}) copy-start(f32[1,2048]{1,0:T(1,128)} %get-tuple-element.224) | copy-start | bytes 24580
  412.8 1.0 copy-start.4
  415.1 267.1 %all-gather.10.cloned.1.call-start = ((), (), s32[]{:S(2)}) async-start(), calls=%async_computation.4 | async-start | bytes 17825792 | tf_op jit(solution)/shard_map/all_gather | solution.py:65
  439.7 6.3 copy-start
  439.7 6.3 copy-start.12
  450.2 0.8 copy-start.2
  450.2 1.0 copy-start.3
  456.0 75.0 %all-to-all-start.1 = ((bf16[2,256,16,128]{3,1,0,2:T(8,128)(2,1)}), bf16[2,256,16,128]{3,1,0,2:T(8,128)(2,1)S(1)}, u32[]{:S(2)}, u32[]{:S(2)}) async-start(bf16[2,256,16,128]{3,1,0,2:T(8,128)(2,1)} %pad_maximum_fusion.1), calls=%async_computation.1 | async-start | bytes 4194304 | tf_op jit(solution)/shard_map/all_to_all | solution.py:76
  462.2 75.8 %copy-start.5 = (bf16[256,16,64]{0,2,1:T(8,128)(2,1)S(1)}, bf16[256,16,64]{0,2,1:T(8,128)(2,1)}, u32[]{:S(2)}) copy-start(bf16[256,16,64]{0,2,1:T(8,128)(2,1)} %get-tuple-element.218) | copy-start | bytes 1572868
  462.2 75.8 %copy-start.6 = (bf16[256,16,64]{0,2,1:T(8,128)(2,1)S(1)}, bf16[256,16,64]{0,2,1:T(8,128)(2,1)}, u32[]{:S(2)}) copy-start(bf16[256,16,64]{0,2,1:T(8,128)(2,1)} %get-tuple-element.219) | copy-start | bytes 1572868
  531.1 66.6 %all-to-all-start = ((bf16[2,256,16,128]{1,3,0,2:T(8,128)(2,1)}), bf16[2,256,16,128]{1,3,0,2:T(8,128)(2,1)}, u32[]{:S(2)}, u32[]{:S(2)}) async-start(bf16[2,256,16,128]{1,3,0,2:T(8,128)(2,1)} %copy.75), calls=%async_computation | async-start | bytes 4194304 | tf_op jit(solution)/shard_map/all_to_all | solution.py:75
  767.1 6.1 copy-start.10
Sparse Core Ops, SparseCore 0:
  70.2 102.9 all-gather.5
  175.4 89.7 all-gather.7
  415.2 155.3 all-gather.11
  572.0 110.0 all-gather.9
where the time goes:
time: 825 us; the launch traced here: 814 us
  waiting for transfers between devices  366 us (44%)
  matrix products  256 us (31%)
  local copies, waits for them, and re-layouts  102 us (12%)
  other arithmetic  39.8 us (5%)
  blocking collectives  22.8 us (3%)
  between operations  14.5 us (2%)
  starting transfers between devices  11.9 us (1%)
    all_gather x2, waiting for transfers between devices, body(): kg = lax.all_gather(k, 'cp', tiled=True)  150 us
    all_gather x2, waiting for transfers between devices, body(): vg = lax.all_gather(v, 'cp', tiled=True)  92 us
    dot_general x32, matrix products, one(): return jnp.dot(p, vh, preferred_element_type=F32).astype(BF16)  71.8 us
    dot_general x32, matrix products, one(): jnp.einsum('qd,kd->qk', qh, kh, preferred_element_type=F32) * HEAD ** (-0.5)  69.9 us
    all_to_all x1, waiting for transfers between devices, body(): vc = _natural(lax.all_to_all(jnp.stack(vl), 'cp', 2, 1, tiled=True), ncp)  67.3 us
    all_to_all x1, waiting for transfers between devices, body(): kc = _natural(lax.all_to_all(jnp.stack(kl), 'cp', 2, 1, tiled=True), ncp)  56.6 us
    dot_general x2, matrix products, body(): jnp.dot(u, w2[l], preferred_element_type=F32)  47.3 us
    dot_general x3, local copies, waits for them, and re-layouts, body(): jnp.dot(h, wq[l], preferred_element_type=F32).reshape(s_dev, nh, HEAD)  36.8 us
  transfers between devices with their start and end apart: 6, of which 5 were waited for; matrix products, arithmetic and copies ran while one was open for 7% of the time, Pallas kernels for 0%

commit v1 on v0

v1 whole, which is shorter than its diff:
```python
import functools

import jax
import jax.numpy as jnp
from jax import lax
from jax.experimental import pallas as pl
from jax.experimental.pallas import tpu as pltpu
from jax.sharding import PartitionSpec as P

HEAD = 128
F32 = jnp.float32
BF16 = jnp.bfloat16
MESH = pl.DeviceIdType.MESH
CORES = 2
QB = 512
KB = 512
FB = 512
SLOTS = 3
SCALE2 = HEAD ** -0.5 * 1.4426950408889634


def _angles(pos):
    half = HEAD // 2
    inv = 1.0 / (10000.0 ** (jnp.arange(half, dtype=F32) * (2.0 / HEAD)))
    ang = pos.astype(F32)[:, None] * inv
    c, sn = jnp.cos(ang), jnp.sin(ang)
    return jnp.concatenate([c, c], axis=-1), jnp.concatenate([-sn, sn], axis=-1)


def _kernel(ncp, x_ref, cos_ref, sin_ref, g1_ref, g2_ref, wq, wk, wv, wo, w1, w3, w2,
            y_ref, kc_ref, vc_ref,
            x_s, h_s, stage, qkv, o_s, o_stage, m_s, l_s, acc_s, y_acc,
            wqkv_s, wo_s, w13_s, w2_s, w13t_s, w2t_s,
            send_sem, recv_sem, osend_sem, orecv_sem,
            wqkv_sem, wo_sem, wm_sem, wt_sem, out_sem):
    n_layers = wq.shape[0]
    rows, dim = x_ref.shape
    seg = rows // 2
    nseg = 2 * ncp
    seq = nseg * seg
    half_seq = seq // 2
    ff = w1.shape[2]
    nf = ff // FB
    tail = ff - nf * FB
    nchip = ncp // CORES
    cw = CORES * HEAD
    me = lax.axis_index("cp")
    req = lax.axis_index("req")
    chip, core = me // CORES, me % CORES
    others = (ncp - 1) * seg

    def chip_at(j):
        off = nchip // 2 + (2 * (j % 2) - 1) * ((j + 1) // 2)
        return lax.rem(chip + off + nchip, nchip)

    def wqkv_copies(g):
        l, j = g // nchip, lax.rem(g, nchip)
        slot = lax.rem(g, 2)
        cols = pl.ds(pl.multiple_of(chip_at(j) * cw, cw), cw)
        return [pltpu.make_async_copy(w.at[l, :, cols], wqkv_s.at[slot, t], wqkv_sem.at[slot])
                for t, w in enumerate((wk, wv, wq))]

    def mlp_copies(l, f, slot):
        cols = pl.ds(pl.multiple_of(f * FB, FB), FB)
        return [pltpu.make_async_copy(w1.at[l, :, cols], w13_s.at[slot, 0], wm_sem.at[slot]),
                pltpu.make_async_copy(w3.at[l, :, cols], w13_s.at[slot, 1], wm_sem.at[slot]),
                pltpu.make_async_copy(w2.at[l, cols, :], w2_s.at[slot], wm_sem.at[slot])]

    def tail_copies(l):
        cols = pl.ds(nf * FB, tail)
        return [pltpu.make_async_copy(w1.at[l, :, cols], w13t_s.at[0], wt_sem),
                pltpu.make_async_copy(w3.at[l, :, cols], w13t_s.at[1], wt_sem),
                pltpu.make_async_copy(w2.at[l, cols, :], w2t_s, wt_sem)]

    def wo_copy(l):
        return pltpu.make_async_copy(wo.at[l], wo_s, wo_sem)

    def start(cs):
        for c in cs:
            c.start()

    def wait(cs):
        for c in cs:
            c.wait()

    def remote(src, dst, ssem, rsem, dev):
        return pltpu.make_async_remote_copy(src_ref=src, dst_ref=dst, send_sem=ssem, recv_sem=rsem,
                                            device_id=(req, dev), device_id_type=MESH)

    def norm(g_ref, l):
        blk = 32

        def body(i, _):
            r = pl.ds(pl.multiple_of(i * blk, blk), blk)
            v = x_s[r, :].astype(F32)
            s = lax.rsqrt(jnp.mean(v * v, axis=-1, keepdims=True) + 1e-5)
            h_s[r, :] = (v * s * g_ref[l]).astype(BF16)
            return 0

        lax.fori_loop(0, rows // blk, body, 0)

    start(wqkv_copies(0))
    start(wqkv_copies(1))
    barrier = pltpu.get_barrier_semaphore()

    def sig(i, _):
        pl.semaphore_signal(barrier, inc=1, device_id=(req, lax.rem(me + 1 + i, ncp)), device_id_type=MESH)
        return 0

    lax.fori_loop(0, ncp - 1, sig, 0)
    x_s[...] = x_ref[...]
    cosv, sinv = cos_ref[...], sin_ref[...]
    row_of = (me * seg, (nseg - 1 - me) * seg)

    def piece(l, j, t, hh, half):
        dev = chip_at(j) * CORES + hh
        r = pl.ds(pl.multiple_of(row_of[half], seg), seg)
        return remote(stage.at[j, t, hh, pl.ds(half * seg, seg), :], qkv.at[l, t, r, :],
                      send_sem.at[l, half, t], recv_sem.at[l, half, t], dev)

    def send_chunk(l, j, half):
        for t in range(3):
            for hh in range(CORES):
                piece(l, j, t, hh, half).start()

    def attend(l, qb, kb, st, masked):
        q = qkv[l, 2, pl.ds(pl.multiple_of(qb * QB, QB), QB), :]
        kr = pl.ds(pl.multiple_of(kb * KB, KB), KB)
        s = lax.dot_general(q, qkv[l, 0, kr, :], (((1,), (1,)), ((), ())), preferred_element_type=F32)
        if masked:
            ri = lax.broadcasted_iota(jnp.int32, (QB, KB), 0)
            ci = lax.broadcasted_iota(jnp.int32, (QB, KB), 1)
            s = jnp.where(ci <= ri, s, -jnp.inf)
        m_old = m_s[st]
        m_new = jnp.maximum(m_old, jnp.max(s, axis=1, keepdims=True))
        mc = m_new * SCALE2
        alpha = jnp.exp2(m_old * SCALE2 - mc)
        ps, tot = [], l_s[st] * alpha
        for c in range(KB // 128):
            p = jnp.exp2(s[:, c * 128:(c + 1) * 128] * SCALE2 - mc)
            tot = tot + p
            ps.append(p.astype(BF16))
        m_s[st] = m_new
        l_s[st] = tot
        pv = jnp.dot(jnp.concatenate(ps, axis=1), qkv[l, 1, kr, :], preferred_element_type=F32)
        acc_s[st] = acc_s[st] * alpha + pv

    def attend_init(st):
        m_s[st] = jnp.full((QB, 128), -jnp.inf, F32)
        l_s[st] = jnp.zeros((QB, 128), F32)
        acc_s[st] = jnp.zeros((QB, HEAD), F32)

    my_cols = pl.ds(pl.multiple_of(me * HEAD, HEAD), HEAD)
    nblk = half_seq // QB

    def finish(l, qb, st, half):
        o = (acc_s[st] / jnp.sum(l_s[st], axis=1, keepdims=True)).astype(BF16)
        o_stage[pl.ds(pl.multiple_of(qb * QB, QB), QB), :] = o
        for i in range(QB // seg):
            s_i = qb * (QB // seg) + i
            dev = s_i if half == 0 else nseg - 1 - s_i

            @pl.when(dev == me)
            def _():
                o_s[l, half * seg:(half + 1) * seg, my_cols] = o[i * seg:(i + 1) * seg]

            @pl.when(dev != me)
            def _():
                remote(o_stage.at[pl.ds(pl.multiple_of(s_i * seg, seg), seg), :],
                       o_s.at[l, pl.ds(half * seg, seg), my_cols],
                       osend_sem.at[l, half], orecv_sem.at[l, half], dev).start()

    def bulk(l, t, ssem, rsem):
        r = qkv.at[l, t, pl.ds(0, others), :]
        return remote(r, r, ssem, rsem, me)

    def mlp_step(a, w13, w2c):
        g = jnp.dot(a, w13[0], preferred_element_type=F32)
        u = jnp.dot(a, w13[1], preferred_element_type=F32)
        u = (g * (1.0 / (1.0 + jnp.exp(-g))) * u).astype(BF16)
        return jnp.dot(u, w2c, preferred_element_type=F32)

    def layer(l, _):
        norm(g1_ref, l)

        def proj(j, _):
            g = l * nchip + j
            slot = lax.rem(g, 2)
            wait(wqkv_copies(g))
            a = h_s[...]
            for t in range(3):
                r = jnp.dot(a, wqkv_s[slot, t], preferred_element_type=F32)
                for hh in range(CORES):
                    v = r[:, hh * HEAD:(hh + 1) * HEAD]
                    if t != 1:
                        v = v * cosv + pltpu.roll(v, HEAD // 2, 1) * sinv
                    stage[j, t, hh] = v.astype(BF16)

            @pl.when(g + 2 < nchip * n_layers)
            def _():
                start(wqkv_copies(g + 2))

            @pl.when(j > 0)
            def _():
                @pl.when(g == 1)
                def _():
                    pl.semaphore_wait(barrier, ncp - 1)
                send_chunk(l, j - 1, 0)
            return 0

        lax.fori_loop(0, nchip, proj, 0)
        last = nchip - 1
        for half in range(2):
            for t in range(3):
                piece(l, last, t, 1 - core, half).start()
            if half == 0:
                def sendb(j, _):
                    send_chunk(l, j, 1)
                    return 0
                lax.fori_loop(0, last, sendb, 0)
        for half in range(2):
            for t in range(3):
                qkv[l, t, pl.ds(pl.multiple_of(row_of[half], seg), seg), :] = \
                    stage[last, t, core, half * seg:(half + 1) * seg, :]
        wo_copy(l).start()
        start(tail_copies(l))
        for f in range(SLOTS):
            start(mlp_copies(l, f, f))

        for t in range(3):
            bulk(l, t, send_sem.at[l, 0, t], recv_sem.at[l, 0, t]).wait_recv()

        def blk_a(qb, _):
            attend_init(qb)
            lax.fori_loop(0, qb, lambda kb, _: (attend(l, qb, kb, qb, False), 0)[1], 0)
            attend(l, qb, qb, qb, True)
            finish(l, qb, qb, 0)
            return 0

        lax.fori_loop(0, nblk, blk_a, 0)
        bulk(l, 2, send_sem.at[l, 1, 2], recv_sem.at[l, 1, 2]).wait_recv()

        def blk_b1(i, _):
            attend_init(i)
            lax.fori_loop(0, nblk, lambda kb, _: (attend(l, nblk + i, kb, i, False), 0)[1], 0)
            return 0

        lax.fori_loop(0, nblk, blk_b1, 0)
        for t in range(2):
            bulk(l, t, send_sem.at[l, 1, t], recv_sem.at[l, 1, t]).wait_recv()
        kc_out = pltpu.make_async_copy(qkv.at[l, 0], kc_ref.at[l], out_sem.at[0])
        vc_out = pltpu.make_async_copy(qkv.at[l, 1], vc_ref.at[l], out_sem.at[1])
        kc_out.start()
        vc_out.start()

        def blk_b2(i, _):
            qb = nblk + i
            lax.fori_loop(nblk, qb, lambda kb, _: (attend(l, qb, kb, i, False), 0)[1], 0)
            attend(l, qb, qb, i, True)
            finish(l, qb, i, 1)
            return 0

        lax.fori_loop(0, nblk, blk_b2, 0)
        for half in range(2):
            for t in range(3):
                bulk(l, t, send_sem.at[l, half, t], recv_sem.at[l, half, t]).wait_send()
        wo_copy(l).wait()
        for half in range(2):
            bulk(l, 0, osend_sem.at[l, half], orecv_sem.at[l, half]).wait_recv()

        def out_proj(c, _):
            cols = pl.ds(pl.multiple_of(c * FB, FB), FB)
            x_s[:, cols] = (x_s[:, cols].astype(F32)
                            + jnp.dot(o_s[l], wo_s[:, cols], preferred_element_type=F32)).astype(BF16)
            return 0

        lax.fori_loop(0, dim // FB, out_proj, 0)
        norm(g2_ref, l)
        wait(tail_copies(l))
        y_acc[...] = mlp_step(h_s[...], w13t_s, w2t_s[...])

        def mlp(f, _):
            slot = lax.rem(f, SLOTS)
            wait(mlp_copies(l, f, slot))
            y_acc[...] += mlp_step(h_s[...], w13_s.at[slot], w2_s[slot])

            @pl.when(f + SLOTS < nf)
            def _():
                start(mlp_copies(l, f + SLOTS, slot))
            return 0

        lax.fori_loop(0, nf, mlp, 0)
        x_s[...] = (x_s[...].astype(F32) + y_acc[...]).astype(BF16)
        kc_out.wait()
        vc_out.wait()
        for half in range(2):
            bulk(l, 0, osend_sem.at[l, half], orecv_sem.at[l, half]).wait_send()
        return 0

    lax.fori_loop(0, n_layers, layer, 0)
    out = pltpu.make_async_copy(x_s, y_ref, out_sem.at[0])
    out.start()
    out.wait()


def solution(mesh):
    ncp = mesh.shape['cp']
    act = P(('req', 'cp'), None)
    cache = P(None, 'req', 'cp', None)

    def body(x, pos, g1, g2, wq, wk, wv, wo, w1, w3, w2):
        rows, dim = x.shape
        n_layers, _, ff = w1.shape
        seq = rows * ncp
        tail = ff % FB
        nchip = ncp // CORES
        cos, sin = _angles(pos)
        gains = [g.astype(F32).reshape(n_layers, 1, dim) for g in (g1, g2)]
        vm = pl.BlockSpec(memory_space=pltpu.VMEM)
        hbm = pl.BlockSpec(memory_space=pl.ANY)
        nb = seq // 2 // QB
        y, kc, vc = pl.pallas_call(
            functools.partial(_kernel, ncp),
            out_shape=(jax.ShapeDtypeStruct((rows, dim), BF16),
                       jax.ShapeDtypeStruct((n_layers, seq, HEAD), BF16),
                       jax.ShapeDtypeStruct((n_layers, seq, HEAD), BF16)),
            in_specs=[vm] * 5 + [hbm] * 7,
            out_specs=(hbm,) * 3,
            scratch_shapes=[
                pltpu.VMEM((rows, dim), BF16),
                pltpu.VMEM((rows, dim), BF16),
                pltpu.VMEM((nchip, 3, CORES, rows, HEAD), BF16),
                pltpu.VMEM((n_layers, 3, seq, HEAD), BF16),
                pltpu.VMEM((n_layers, rows, ncp * HEAD), BF16),
                pltpu.VMEM((seq, HEAD), BF16),
                pltpu.VMEM((nb, QB, 128), F32),
                pltpu.VMEM((nb, QB, 128), F32),
                pltpu.VMEM((nb, QB, HEAD), F32),
                pltpu.VMEM((rows, dim), F32),
                pltpu.VMEM((2, 3, dim, CORES * HEAD), BF16),
                pltpu.VMEM((ncp * HEAD, dim), BF16),
                pltpu.VMEM((SLOTS, 2, dim, FB), BF16),
                pltpu.VMEM((SLOTS, FB, dim), BF16),
                pltpu.VMEM((2, dim, tail), BF16),
                pltpu.VMEM((tail, dim), BF16),
                pltpu.SemaphoreType.DMA((n_layers, 2, 3)),
                pltpu.SemaphoreType.DMA((n_layers, 2, 3)),
                pltpu.SemaphoreType.DMA((n_layers, 2)),
                pltpu.SemaphoreType.DMA((n_layers, 2)),
                pltpu.SemaphoreType.DMA((2,)),
                pltpu.SemaphoreType.DMA,
                pltpu.SemaphoreType.DMA((SLOTS,)),
                pltpu.SemaphoreType.DMA,
                pltpu.SemaphoreType.DMA((2,)),
            ],
            compiler_params=pltpu.CompilerParams(collective_id=0, has_side_effects=True,
                                                 vmem_limit_bytes=67043328),
        )(x, cos, sin, *gains, wq, wk, wv, wo, w1, w3, w2)
        return y, kc[:, :, None, :], vc[:, :, None, :]

    return jax.shard_map(body, mesh=mesh, in_specs=(act, P(('req', 'cp'))) + (P(),) * 9,
                         out_specs=(act, cache, cache), check_vma=False)
```

time: 825 us -> 281 us (0.34); the launches traced: 814 us -> 281 us
  waiting for transfers between devices: 366 us -> 0 us
  Pallas kernels: 0 us -> 267 us
  matrix products: 256 us -> 0 us
  local copies, waits for them, and re-layouts: 102 us -> 11 us
  other arithmetic: 39.8 us -> 2.07 us
  blocking collectives: 22.8 us -> 0 us
  between operations: 14.5 us -> 0.65 us
  starting transfers between devices: 11.9 us -> 0 us
    pallas_call x0 -> x1, Pallas kernels: none -> 267 us  [body(): pl.pallas_call(functools.partial(_kernel, ncp), out_shape=(jax.ShapeDtype...]
    dot_general x76 -> x0, matrix products: 256 us -> none  [the longest x32 71.8 us: one(): return jnp.dot(p, vh, preferred_element_type=F32).astype(BF16)]
    all_gather x4 -> x0, waiting for transfers between devices: 242 us -> none  [the longest x2 150 us: body(): kg = lax.all_gather(k, 'cp', tiled=True)]
    all_to_all x2 -> x0, waiting for transfers between devices: 124 us -> none  [the longest x1 67.3 us: body(): vc = _natural(lax.all_to_all(jnp.stack(vl), 'cp', 2, 1, tiled=True), ncp)]
    dot_general x6 -> x0, local copies, waits for them, and re-layouts: 73.1 us -> none  [the longest x3 36.8 us: body(): jnp.dot(h, wq[l], preferred_element_type=F32).reshape(s_dev, nh, HEAD)]
    reduce_sum x33 -> x0, other arithmetic: 24.4 us -> none  [the longest x32 22.9 us: one(): p = jax.nn.softmax(jnp.where(mask, sc, -jnp.inf), axis=-1).astype(BF16)]
    all_gather x1 -> x0, blocking collectives: 22.8 us -> none  [body(): pos_all = lax.all_gather(pos, 'cp', tiled=True)]
    dynamic_update_slice x64 -> x0, local copies, waits for them, and re-layouts: 13.8 us -> none  [_attention(): lax.map(one, (q.transpose(1, 0, 2), kg.transpose(1, 0, 2), vg.transpose(1...]
  transfers between devices with their start and end apart: 6 -> 0, of which waited for: 5 -> 0; matrix products, arithmetic and copies ran while one was open for 7% -> 0% of each run, Pallas kernels for 0% -> 0%
where the time goes in v1:
time: 281 us
  Pallas kernels  267 us (95%)
  local copies, waits for them, and re-layouts  11 us (4%)
    pallas_call x1, Pallas kernels, body(): pl.pallas_call(functools.partial(_kernel, ncp), out_shape=(jax.ShapeDtype...  267 us
    unnamed x3, local copies, waits for them, and re-layouts  8.39 us

profile of v1, /device:TPU:21, one launch (start us, length us, event | category | flops | bytes accessed | tf_op | source)
XLA Modules:
  0.0 281.1 jit_solution(3183375046092837526)
XLA Ops:
  0.6 0.7 convert_element_type.2
  1.3 1.3 reshape.28.g1_ref
  2.6 1.3 reshape.30.g2_ref
  4.0 0.5 fusion
  4.5 0.8 pad_maximum_fusion
  5.3 267.4 %shard_map.130 = (bf16[256,2048]{1,0:T(8,128)(2,1)}, bf16[2,4096,128]{2,1,0:T(8,128)(2,1)}, bf16[2,4096,128]{2,1,0:T(8,128)(2,1)}) custom-call(bf16[256,2048]{1,0:T(8,128)(2,1)} %x_ref.1, f32[256,128]{1,0:T(8,128)} %get-tuple-element.15.cos_ref, f32[256,128]{1,0:T(8,128)} %get-tuple-element.16.sin_ref, f32[2,1,2048]{2,1,0:T(1,128)} %reshape.28.g1_ref, ...), custom_call_target="tpu_custom_call" | custom-call | tf_op jit(solution)/shard_map/pallas_call | solution.py:322
  272.7 2.3 copy.19
  275.1 3.0 %copy.20 = bf16[2,4096,1,128]{3,1,2,0:T(8,128)(2,1)} copy(bf16[2,4096,1,128]{3,1,2,0:T(8,128)(2,1)} %bitcast.7) | data formatting | bytes 4194304
  278.1 3.0 %copy.21 = bf16[2,4096,1,128]{3,1,2,0:T(8,128)(2,1)} copy(bf16[2,4096,1,128]{3,1,2,0:T(8,128)(2,1)} %bitcast.6) | data formatting | bytes 4194304
  (1 shorter events, 0.0 us)

commit v2 on v1

v2 whole, which is shorter than its diff:
```python
import functools

import jax
import jax.numpy as jnp
from jax import lax
from jax.experimental import pallas as pl
from jax.experimental.pallas import tpu as pltpu
from jax.sharding import PartitionSpec as P

HEAD = 128
F32 = jnp.float32
BF16 = jnp.bfloat16
MESH = pl.DeviceIdType.MESH
CORES = 2
QB = 512
KB = 512
FB = 512
SLOTS = 3
SCALE2 = HEAD ** -0.5 * 1.4426950408889634


def _angles(pos):
    half = HEAD // 2
    inv = 1.0 / (10000.0 ** (jnp.arange(half, dtype=F32) * (2.0 / HEAD)))
    ang = pos.astype(F32)[:, None] * inv
    c, sn = jnp.cos(ang), jnp.sin(ang)
    return jnp.concatenate([c, c], axis=-1), jnp.concatenate([-sn, sn], axis=-1)


def _kernel(ncp, x_ref, cos_ref, sin_ref, g1_ref, g2_ref, wq, wk, wv, wo, w1, w3, w2,
            y_ref, kc_ref, vc_ref,
            x_s, h_s, stage, qkv, o_s, o_stage, m_s, l_s, acc_s, y_acc, relay,
            wqkv_s, wo_s, w13_s, w2_s, w13t_s, w2t_s,
            send_sem, recv_sem, osend_sem, orecv_sem, rrecv_sem, fsend_sem,
            wqkv_sem, wo_sem, wm_sem, wt_sem, out_sem):
    n_layers = wq.shape[0]
    rows, dim = x_ref.shape
    seg = rows // 2
    nseg = 2 * ncp
    seq = nseg * seg
    half_seq = seq // 2
    ff = w1.shape[2]
    nf = ff // FB
    tail = ff - nf * FB
    nchip = ncp // CORES
    last = nchip - 1
    cw = CORES * HEAD
    me = lax.axis_index("cp")
    req = lax.axis_index("req")
    chip, core = me // CORES, me % CORES
    others = (ncp - 1) * seg
    qpasses = [(0, 2)] + [(l, h) for l in range(1, n_layers) for h in range(2)]
    mpasses = [(l, h) for l in range(n_layers - 1) for h in range(2)] + [(n_layers - 1, 2)]
    part = (slice(0, seg), slice(seg, rows), slice(0, rows))

    def chip_at(j):
        off = nchip // 2 + (2 * (j % 2) - 1) * ((j + 1) // 2)
        return lax.rem(chip + off + nchip, nchip)

    def wqkv_copies(p, j):
        slot = (p * nchip + j) % 2 if isinstance(j, int) else lax.rem(p * nchip + j, 2)
        cols = pl.ds(pl.multiple_of(chip_at(j) * cw, cw), cw)
        return [pltpu.make_async_copy(w.at[qpasses[p][0], :, cols], wqkv_s.at[slot, t], wqkv_sem.at[slot])
                for t, w in enumerate((wk, wv, wq))]

    def mlp_copies(p, f, slot):
        l = mpasses[p][0]
        cols = pl.ds(pl.multiple_of(f * FB, FB), FB)
        return [pltpu.make_async_copy(w1.at[l, :, cols], w13_s.at[slot, 0], wm_sem.at[slot]),
                pltpu.make_async_copy(w3.at[l, :, cols], w13_s.at[slot, 1], wm_sem.at[slot]),
                pltpu.make_async_copy(w2.at[l, cols, :], w2_s.at[slot], wm_sem.at[slot])]

    def tail_copies(l):
        cols = pl.ds(nf * FB, tail)
        return [pltpu.make_async_copy(w1.at[l, :, cols], w13t_s.at[0], wt_sem),
                pltpu.make_async_copy(w3.at[l, :, cols], w13t_s.at[1], wt_sem),
                pltpu.make_async_copy(w2.at[l, cols, :], w2t_s, wt_sem)]

    def wo_copies(l):
        return [pltpu.make_async_copy(wo.at[l], wo_s, wo_sem)]

    def start(cs):
        for c in cs:
            c.start()

    def wait(cs):
        for c in cs:
            c.wait()

    def remote(src, dst, ssem, rsem, dev):
        return pltpu.make_async_remote_copy(src_ref=src, dst_ref=dst, send_sem=ssem, recv_sem=rsem,
                                            device_id=(req, dev), device_id_type=MESH)

    def norm(g_ref, l, h):
        blk = 32
        first = part[h].start // blk

        def body(i, _):
            r = pl.ds(pl.multiple_of(i * blk, blk), blk)
            v = x_s[r, :].astype(F32)
            s = lax.rsqrt(jnp.mean(v * v, axis=-1, keepdims=True) + 1e-5)
            h_s[r, :] = (v * s * g_ref[l:l + 1, :].astype(F32)).astype(BF16)
            return 0

        lax.fori_loop(first, part[h].stop // blk, body, 0)

    start(wqkv_copies(0, 0))
    start(wqkv_copies(0, 1))
    barrier = pltpu.get_barrier_semaphore()

    def sig(i, _):
        pl.semaphore_signal(barrier, inc=1, device_id=(req, lax.rem(me + 1 + i, ncp)), device_id_type=MESH)
        return 0

    lax.fori_loop(0, ncp - 1, sig, 0)
    x_s[...] = x_ref[...]

    def row_of(dev, half):
        r = dev * seg if half == 0 else (nseg - 1 - dev) * seg
        return pl.ds(pl.multiple_of(r, seg), seg)

    def piece(l, j, t, hh, half):
        dev = chip_at(j) * CORES + hh
        return remote(stage.at[j, t, hh, pl.ds(half * seg, seg), :], qkv.at[l, t, row_of(me, half), :],
                      send_sem.at[l, half, t], recv_sem.at[l, half, t], dev)

    hop = nchip // 4

    def via(half, sign):
        step = hop if half == 0 else nchip - hop
        return lax.rem(chip + (step if sign > 0 else nchip - step), nchip)

    def send_far(l, half):
        for t in range(3):
            for hh in range(CORES):
                remote(stage.at[0, t, hh, pl.ds(half * seg, seg), :], relay.at[l, half, t, hh],
                       send_sem.at[l, half, t], rrecv_sem.at[l, half], via(half, 1) * CORES + core).start()

    def forward(l, half):
        buf = relay.at[l, half]
        remote(buf, buf, fsend_sem.at[l, half], rrecv_sem.at[l, half], me).wait_recv()
        src = via(half, -1) * CORES + core
        for t in range(3):
            for hh in range(CORES):
                remote(relay.at[l, half, t, hh], qkv.at[l, t, row_of(src, half), :],
                       fsend_sem.at[l, half], recv_sem.at[l, half, t], via(half, 1) * CORES + hh).start()

    def forward_sent(l, half):
        buf = relay.at[l, half]
        remote(buf, buf, fsend_sem.at[l, half], rrecv_sem.at[l, half], me).wait_send()

    def send_chunk(l, j, half, ts=(0, 1, 2)):
        for t in ts:
            for hh in range(CORES):
                piece(l, j, t, hh, half).start()

    def send_sibling(l, half, ts=(0, 1, 2)):
        for t in ts:
            piece(l, last, t, 1 - core, half).start()

    def send_rest(l, half, ts):
        lax.fori_loop(1, last, lambda j, _: (send_chunk(l, j, half, ts), 0)[1], 0)
        send_sibling(l, half, ts)

    def keep_own(l, half):
        for t in range(3):
            qkv[l, t, row_of(me, half), :] = stage[last, t, core, half * seg:(half + 1) * seg, :]

    def project(p):
        l, h = qpasses[p]
        sl = part[h]
        cosv, sinv = cos_ref[sl, :], sin_ref[sl, :]

        def body(j, _):
            slot = lax.rem(p * nchip + j, 2)
            wait(wqkv_copies(p, j))
            a = h_s[sl, :]
            for t in range(3):
                r = jnp.dot(a, wqkv_s[slot, t], preferred_element_type=F32)
                for hh in range(CORES):
                    v = r[:, hh * HEAD:(hh + 1) * HEAD]
                    if t != 1:
                        v = v * cosv + pltpu.roll(v, HEAD // 2, 1) * sinv
                    stage[j, t, hh, sl, :] = v.astype(BF16)

            @pl.when(j + 2 < nchip)
            def _():
                start(wqkv_copies(p, j + 2))

            if p + 1 < len(qpasses):
                @pl.when(j + 2 >= nchip)
                def _():
                    start(wqkv_copies(p + 1, j + 2 - nchip))

            @pl.when(j == 1)
            def _():
                if p == 0:
                    pl.semaphore_wait(barrier, ncp - 1)
                for half in ((0, 1) if h == 2 else (h,)):
                    send_far(l, half)

            @pl.when(j > 1)
            def _():
                send_chunk(l, j - 1, 0 if h == 2 else h)
            return 0

        lax.fori_loop(0, nchip, body, 0)
        send_sibling(l, 0 if h == 2 else h)
        for half in ((0, 1) if h == 2 else (h,)):
            keep_own(l, half)

    def attend(l, qb, kb, st, masked):
        q = qkv[l, 2, pl.ds(pl.multiple_of(qb * QB, QB), QB), :]
        kr = pl.ds(pl.multiple_of(kb * KB, KB), KB)
        s = lax.dot_general(q, qkv[l, 0, kr, :], (((1,), (1,)), ((), ())), preferred_element_type=F32)
        if masked:
            ri = lax.broadcasted_iota(jnp.int32, (QB, KB), 0)
            ci = lax.broadcasted_iota(jnp.int32, (QB, KB), 1)
            s = jnp.where(ci <= ri, s, -jnp.inf)
        m_old = m_s[st]
        m_new = jnp.maximum(m_old, jnp.max(s, axis=1, keepdims=True))
        mc = m_new * SCALE2
        alpha = jnp.exp2(m_old * SCALE2 - mc)
        ps, tot = [], l_s[st] * alpha
        for c in range(KB // 128):
            p = jnp.exp2(s[:, c * 128:(c + 1) * 128] * SCALE2 - mc)
            tot = tot + p
            ps.append(p.astype(BF16))
        m_s[st] = m_new
        l_s[st] = tot
        pv = jnp.dot(jnp.concatenate(ps, axis=1), qkv[l, 1, kr, :], preferred_element_type=F32)
        acc_s[st] = acc_s[st] * alpha + pv

    def attend_init(st):
        m_s[st] = jnp.full((QB, 128), -jnp.inf, F32)
        l_s[st] = jnp.zeros((QB, 128), F32)
        acc_s[st] = jnp.zeros((QB, HEAD), F32)

    my_cols = pl.ds(pl.multiple_of(me * HEAD, HEAD), HEAD)
    nblk = half_seq // QB

    def finish(l, qb, st, half):
        o = (acc_s[st] / jnp.sum(l_s[st], axis=1, keepdims=True)).astype(BF16)
        o_stage[pl.ds(pl.multiple_of(qb * QB, QB), QB), :] = o
        for i in range(QB // seg):
            s_i = qb * (QB // seg) + i
            dev = s_i if half == 0 else nseg - 1 - s_i

            @pl.when(dev == me)
            def _():
                o_s[l, half * seg:(half + 1) * seg, my_cols] = o[i * seg:(i + 1) * seg]

            @pl.when(dev != me)
            def _():
                remote(o_stage.at[pl.ds(pl.multiple_of(s_i * seg, seg), seg), :],
                       o_s.at[l, pl.ds(half * seg, seg), my_cols],
                       osend_sem.at[l, half], orecv_sem.at[l, half], dev).start()

    def attend_a(l):
        def body(qb, _):
            attend_init(qb)
            lax.fori_loop(0, qb, lambda kb, _: (attend(l, qb, kb, qb, False), 0)[1], 0)
            attend(l, qb, qb, qb, True)
            finish(l, qb, qb, 0)
            return 0

        lax.fori_loop(0, nblk, body, 0)

    def attend_ba(l):
        def body(i, _):
            attend_init(i)
            lax.fori_loop(0, nblk, lambda kb, _: (attend(l, nblk + i, kb, i, False), 0)[1], 0)
            return 0

        lax.fori_loop(0, nblk, body, 0)

    def attend_bb(l):
        def body(i, _):
            qb = nblk + i
            lax.fori_loop(nblk, qb, lambda kb, _: (attend(l, qb, kb, i, False), 0)[1], 0)
            attend(l, qb, qb, i, True)
            finish(l, qb, i, 1)
            return 0

        lax.fori_loop(0, nblk, body, 0)

    def bulk(l, t, ssem, rsem):
        r = qkv.at[l, t, pl.ds(0, others), :]
        return remote(r, r, ssem, rsem, me)

    def recv(l, half, ts):
        for t in ts:
            bulk(l, t, send_sem.at[l, half, t], recv_sem.at[l, half, t]).wait_recv()

    def sent(l, half):
        for t in range(3):
            bulk(l, t, send_sem.at[l, half, t], recv_sem.at[l, half, t]).wait_send()
        forward_sent(l, half)

    def o_recv(l, half):
        bulk(l, 0, osend_sem.at[l, half], orecv_sem.at[l, half]).wait_recv()

    def o_sent(l, half):
        bulk(l, 0, osend_sem.at[l, half], orecv_sem.at[l, half]).wait_send()

    def mlp_step(a, w13, w2c):
        g = jnp.dot(a, w13[0], preferred_element_type=F32)
        u = jnp.dot(a, w13[1], preferred_element_type=F32)
        u = (g * (1.0 / (1.0 + jnp.exp(-g))) * u).astype(BF16)
        return jnp.dot(u, w2c, preferred_element_type=F32)

    def dense(p, midway=None):
        l, h = mpasses[p]
        sl = part[h]
        reload = p + 1 < len(mpasses) and mpasses[p + 1][0] != l
        first = p == 0 or mpasses[p - 1][0] != l
        if first:
            wait(wo_copies(l))

        def out_proj(c, _):
            cols = pl.ds(pl.multiple_of(c * FB, FB), FB)
            x_s[sl, cols] = (x_s[sl, cols].astype(F32)
                             + jnp.dot(o_s[l, sl, :], wo_s[:, cols], preferred_element_type=F32)).astype(BF16)
            return 0

        lax.fori_loop(0, dim // FB, out_proj, 0)
        if reload:
            start(wo_copies(l + 1))
        norm(g2_ref, l, h)
        if first:
            wait(tail_copies(l))
        y_acc[sl, :] = mlp_step(h_s[sl, :], w13t_s, w2t_s[...])
        if reload:
            start(tail_copies(l + 1))

        def body(f, _):
            slot = lax.rem(p * nf + f, SLOTS)
            wait(mlp_copies(p, f, slot))
            y_acc[sl, :] += mlp_step(h_s[sl, :], w13_s.at[slot], w2_s[slot])

            @pl.when(f + SLOTS < nf)
            def _():
                start(mlp_copies(p, f + SLOTS, slot))

            if p + 1 < len(mpasses):
                @pl.when(f + SLOTS >= nf)
                def _():
                    start(mlp_copies(p + 1, f + SLOTS - nf, slot))

            if midway is not None:
                pl.when(f == nf // 2)(midway)
            return 0

        lax.fori_loop(0, nf, body, 0)
        x_s[sl, :] = (x_s[sl, :].astype(F32) + y_acc[sl, :]).astype(BF16)

    norm(g1_ref, 0, 2)
    project(0)
    send_rest(0, 1, (2,))
    start(wo_copies(0))
    start(tail_copies(0))
    for f in range(SLOTS):
        start(mlp_copies(0, f, f))
    forward(0, 0)
    forward(0, 1)
    outs = []
    for l in range(n_layers):
        if l > 0:
            o_sent(l - 1, 0)
        recv(l, 0, (0, 1, 2))
        attend_a(l)
        if l == 0:
            send_rest(l, 1, (0, 1))
        else:
            forward(l, 1)
        recv(l, 1, (2,))
        attend_ba(l)
        more = l + 1 < n_layers
        if more:
            o_recv(l, 0)
            dense(2 * l)
            norm(g1_ref, l + 1, 0)
        if l > 0:
            o_sent(l - 1, 1)
        recv(l, 1, (0, 1))
        for i, c in enumerate((kc_ref, vc_ref)):
            cp = pltpu.make_async_copy(qkv.at[l, i], c.at[l], out_sem.at[l, i])
            cp.start()
            outs.append(cp)
        attend_bb(l)
        sent(l, 0)
        if more:
            project(2 * l + 1)
            o_recv(l, 1)
            dense(2 * l + 1, midway=lambda: forward(l + 1, 0))
            norm(g1_ref, l + 1, 1)
            sent(l, 1)
            project(2 * l + 2)
        else:
            sent(l, 1)
            o_recv(l, 0)
            o_recv(l, 1)
            dense(2 * l)
            o_sent(l, 0)
            o_sent(l, 1)
    wait(outs)
    out = pltpu.make_async_copy(x_s, y_ref, out_sem.at[0, 0])
    out.start()
    out.wait()


def _copy_kernel(*refs):
    n = len(refs) // 3
    ins, outs, bufs, rsem, wsem = refs[:n], refs[n:2 * n], refs[2 * n:3 * n], refs[3 * n], refs[3 * n + 1]
    jobs = []
    for a, b, buf in zip(ins, outs, bufs):
        for i in range(a.shape[0]):
            jobs.append((pltpu.make_async_copy(a.at[i], buf.at[i], rsem.at[len(jobs)]),
                         pltpu.make_async_copy(buf.at[i], b.at[i], wsem.at[len(jobs)])))
    for r, _ in jobs:
        r.start()
    for r, w in jobs:
        r.wait()
        w.start()
    for _, w in jobs:
        w.wait()


def _settle(*arrays):
    hbm = pl.BlockSpec(memory_space=pl.ANY)
    n = sum(a.shape[0] for a in arrays)
    return pl.pallas_call(
        _copy_kernel,
        out_shape=tuple(jax.ShapeDtypeStruct(a.shape, a.dtype) for a in arrays),
        in_specs=[hbm] * len(arrays),
        out_specs=(hbm,) * len(arrays),
        scratch_shapes=[pltpu.VMEM(a.shape, a.dtype) for a in arrays]
        + [pltpu.SemaphoreType.DMA((n,)), pltpu.SemaphoreType.DMA((n,))],
    )(*arrays)


def solution(mesh):
    ncp = mesh.shape['cp']
    act = P(('req', 'cp'), None)
    cache = P(None, 'req', 'cp', None)

    def body(x, pos, g1, g2, wq, wk, wv, wo, w1, w3, w2):
        rows, dim = x.shape
        n_layers, _, ff = w1.shape
        seq = rows * ncp
        tail = ff % FB
        nchip = ncp // CORES
        cos, sin = _angles(pos)
        vm = pl.BlockSpec(memory_space=pltpu.VMEM)
        hbm = pl.BlockSpec(memory_space=pl.ANY)
        nb = seq // 2 // QB
        y, kc, vc = pl.pallas_call(
            functools.partial(_kernel, ncp),
            out_shape=(jax.ShapeDtypeStruct((rows, dim), BF16),
                       jax.ShapeDtypeStruct((n_layers, seq, HEAD), BF16),
                       jax.ShapeDtypeStruct((n_layers, seq, HEAD), BF16)),
            in_specs=[vm] * 5 + [hbm] * 7,
            out_specs=(hbm,) * 3,
            scratch_shapes=[
                pltpu.VMEM((rows, dim), BF16),
                pltpu.VMEM((rows, dim), BF16),
                pltpu.VMEM((nchip, 3, CORES, rows, HEAD), BF16),
                pltpu.VMEM((n_layers, 3, seq, HEAD), BF16),
                pltpu.VMEM((n_layers, rows, ncp * HEAD), BF16),
                pltpu.VMEM((seq, HEAD), BF16),
                pltpu.VMEM((nb, QB, 128), F32),
                pltpu.VMEM((nb, QB, 128), F32),
                pltpu.VMEM((nb, QB, HEAD), F32),
                pltpu.VMEM((rows, dim), F32),
                pltpu.VMEM((n_layers, 2, 3, CORES, rows // 2, HEAD), BF16),
                pltpu.VMEM((2, 3, dim, CORES * HEAD), BF16),
                pltpu.VMEM((ncp * HEAD, dim), BF16),
                pltpu.VMEM((SLOTS, 2, dim, FB), BF16),
                pltpu.VMEM((SLOTS, FB, dim), BF16),
                pltpu.VMEM((2, dim, tail), BF16),
                pltpu.VMEM((tail, dim), BF16),
                pltpu.SemaphoreType.DMA((n_layers, 2, 3)),
                pltpu.SemaphoreType.DMA((n_layers, 2, 3)),
                pltpu.SemaphoreType.DMA((n_layers, 2)),
                pltpu.SemaphoreType.DMA((n_layers, 2)),
                pltpu.SemaphoreType.DMA((n_layers, 2)),
                pltpu.SemaphoreType.DMA((n_layers, 2)),
                pltpu.SemaphoreType.DMA((2,)),
                pltpu.SemaphoreType.DMA,
                pltpu.SemaphoreType.DMA((SLOTS,)),
                pltpu.SemaphoreType.DMA,
                pltpu.SemaphoreType.DMA((n_layers, 2)),
            ],
            compiler_params=pltpu.CompilerParams(collective_id=0, has_side_effects=True,
                                                 vmem_limit_bytes=67043328),
        )(x, cos, sin, g1, g2, wq, wk, wv, wo, w1, w3, w2)
        y, kc, vc = _settle(y.reshape(2, rows // 2, dim), kc, vc)
        return y.reshape(rows, dim), kc[:, :, None, :], vc[:, :, None, :]

    return jax.shard_map(body, mesh=mesh, in_specs=(act, P(('req', 'cp'))) + (P(),) * 9,
                         out_specs=(act, cache, cache), check_vma=False)
```

time: 281 us -> 269 us (0.957)
  local copies, waits for them, and re-layouts: 11 us -> 0 us
    unnamed x3 -> x0, local copies, waits for them, and re-layouts: 8.39 us -> none
    pallas_call x1, Pallas kernels: 267 us -> 261 us  [body(): pl.pallas_call(functools.partial(_kernel, ncp), out_shape=(jax.ShapeDtype...]
    pallas_call x0 -> x1, Pallas kernels: none -> 4.71 us  [_settle(): pl.pallas_call(_copy_kernel, out_shape=tuple((jax.ShapeDtypeStruct(a.shap...]
where the time goes in v2:
time: 269 us
  Pallas kernels  266 us (99%)
    pallas_call x1, Pallas kernels, body(): pl.pallas_call(functools.partial(_kernel, ncp), out_shape=(jax.ShapeDtype...  261 us

profile of v2, /device:TPU:21, one launch (start us, length us, event | category | flops | bytes accessed | tf_op | source)
XLA Modules:
  0.0 268.5 jit_solution(14571883190082173841)
XLA Ops:
  0.6 0.7 convert_element_type.3
  1.3 0.5 fusion
  1.9 0.8 pad_maximum_fusion
  2.7 260.9 %shard_map.130 = (bf16[256,2048]{1,0:T(8,128)(2,1)}, bf16[2,4096,128]{2,1,0:T(8,128)(2,1)}, bf16[2,4096,128]{2,1,0:T(8,128)(2,1)}) custom-call(bf16[256,2048]{1,0:T(8,128)(2,1)} %x_ref.1, f32[256,128]{1,0:T(8,128)} %get-tuple-element.21.cos_ref, f32[256,128]{1,0:T(8,128)} %get-tuple-element.22.sin_ref, bf16[2,2048]{1,0:T(2,128)(2,1)} %g1_ref.1, ...), custom_call_target="tpu_custom_call" | custom-call | tf_op jit(solution)/shard_map/pallas_call | solution.py:457
  263.6 4.7 %shard_map.131 = (bf16[2,128,2048]{2,1,0:T(8,128)(2,1)}, bf16[2,4096,128]{2,1,0:T(8,128)(2,1)}, bf16[2,4096,128]{2,1,0:T(8,128)(2,1)}) custom-call(bf16[2,128,2048]{2,1,0:T(8,128)(2,1)} %bitcast.8, bf16[2,4096,128]{2,1,0:T(8,128)(2,1)} %get-tuple-element.10.refs_1_, bf16[2,4096,128]{2,1,0:T(8,128)(2,1)} %get-tuple-element.11.refs_2_), custom_call_target="tpu_custom_call" | custom-call | tf_op jit(solution)/shard_map/pallas_call | solution.py:432
  (1 shorter events, 0.0 us)

commit v3 on v2

--- a/solution.py
+++ b/solution.py
@@ -31,7 +31,7 @@
             y_ref, kc_ref, vc_ref,
             x_s, h_s, stage, qkv, o_s, o_stage, m_s, l_s, acc_s, y_acc, relay,
             wqkv_s, wo_s, w13_s, w2_s, w13t_s, w2t_s,
-            send_sem, recv_sem, osend_sem, orecv_sem, rrecv_sem, fsend_sem,
+            send_sem, recv_sem, osend_sem, orecv_sem, rsend_sem, rrecv_sem, fsend_sem,
             wqkv_sem, wo_sem, wm_sem, wt_sem, out_sem):
     n_layers = wq.shape[0]
     rows, dim = x_ref.shape
@@ -119,52 +119,50 @@
         r = dev * seg if half == 0 else (nseg - 1 - dev) * seg
         return pl.ds(pl.multiple_of(r, seg), seg)
 
-    def piece(l, j, t, hh, half):
+    A_ALL, B_KV, B_Q = (0, slice(0, 3), 0), (1, slice(0, 2), 1), (1, slice(2, 3), 2)
+
+    def piece(l, j, hh, what):
+        half, ts, sem = what
         dev = chip_at(j) * CORES + hh
-        return remote(stage.at[j, t, hh, pl.ds(half * seg, seg), :], qkv.at[l, t, row_of(me, half), :],
-                      send_sem.at[l, half, t], recv_sem.at[l, half, t], dev)
-
-    hop = nchip // 4
-
-    def via(half, sign):
-        step = hop if half == 0 else nchip - hop
-        return lax.rem(chip + (step if sign > 0 else nchip - step), nchip)
+        return remote(stage.at[j, hh, ts, pl.ds(half * seg, seg), :], qkv.at[l, ts, row_of(me, half), :],
+                      send_sem.at[l, sem], recv_sem.at[l, sem], dev)
+
+    def hops(hh, sign):
+        step = (nchip // 4) if (hh == 0) == (sign > 0) else nchip - nchip // 4
+        return lax.rem(chip + step, nchip)
+
+    def far_copy(l, half, hh):
+        return remote(stage.at[0, hh, :, pl.ds(half * seg, seg), :], relay.at[l, half, hh],
+                      rsend_sem.at[l, half, hh], rrecv_sem.at[l, half, hh], hops(hh, 1) * CORES + core)
 
     def send_far(l, half):
-        for t in range(3):
-            for hh in range(CORES):
-                remote(stage.at[0, t, hh, pl.ds(half * seg, seg), :], relay.at[l, half, t, hh],
-                       send_sem.at[l, half, t], rrecv_sem.at[l, half], via(half, 1) * CORES + core).start()
+        for hh in range(CORES):
+            far_copy(l, half, hh).start()
+
+    def forward_copies(l, half, hh):
+        src = hops(hh, -1) * CORES + core
+        return [remote(relay.at[l, half, hh, ts], qkv.at[l, ts, row_of(src, half), :],
+                       fsend_sem.at[l, half, hh, i], recv_sem.at[l, sem], hops(hh, 1) * CORES + hh)
+                for i, (_, ts, sem) in enumerate((A_ALL,) if half == 0 else (B_Q, B_KV))]
 
     def forward(l, half):
-        buf = relay.at[l, half]
-        remote(buf, buf, fsend_sem.at[l, half], rrecv_sem.at[l, half], me).wait_recv()
-        src = via(half, -1) * CORES + core
-        for t in range(3):
-            for hh in range(CORES):
-                remote(relay.at[l, half, t, hh], qkv.at[l, t, row_of(src, half), :],
-                       fsend_sem.at[l, half], recv_sem.at[l, half, t], via(half, 1) * CORES + hh).start()
-
-    def forward_sent(l, half):
-        buf = relay.at[l, half]
-        remote(buf, buf, fsend_sem.at[l, half], rrecv_sem.at[l, half], me).wait_send()
-
-    def send_chunk(l, j, half, ts=(0, 1, 2)):
-        for t in ts:
-            for hh in range(CORES):
-                piece(l, j, t, hh, half).start()
-
-    def send_sibling(l, half, ts=(0, 1, 2)):
-        for t in ts:
-            piece(l, last, t, 1 - core, half).start()
-
-    def send_rest(l, half, ts):
-        lax.fori_loop(1, last, lambda j, _: (send_chunk(l, j, half, ts), 0)[1], 0)
-        send_sibling(l, half, ts)
+        for hh in range(CORES):
+            far_copy(l, half, hh).wait_recv()
+            start(forward_copies(l, half, hh))
+
+    def send_chunk(l, j, what):
+        for hh in range(CORES):
+            piece(l, j, hh, what).start()
+
+    def send_sibling(l, what):
+        piece(l, last, 1 - core, what).start()
+
+    def send_rest(l, what):
+        lax.fori_loop(1, last, lambda j, _: (send_chunk(l, j, what), 0)[1], 0)
+        send_sibling(l, what)
 
     def keep_own(l, half):
-        for t in range(3):
-            qkv[l, t, row_of(me, half), :] = stage[last, t, core, half * seg:(half + 1) * seg, :]
+        qkv[l, :, row_of(me, half), :] = stage[last, core, :, half * seg:(half + 1) * seg, :]
 
     def project(p):
         l, h = qpasses[p]
@@ -181,7 +179,7 @@
                     v = r[:, hh * HEAD:(hh + 1) * HEAD]
                     if t != 1:
                         v = v * cosv + pltpu.roll(v, HEAD // 2, 1) * sinv
-                    stage[j, t, hh, sl, :] = v.astype(BF16)
+                    stage[j, hh, t, sl, :] = v.astype(BF16)
 
             @pl.when(j + 2 < nchip)
             def _():
@@ -196,16 +194,17 @@
             def _():
                 if p == 0:
                     pl.semaphore_wait(barrier, ncp - 1)
-                for half in ((0, 1) if h == 2 else (h,)):
-                    send_far(l, half)
+                send_far(l, 0 if h == 2 else h)
 
             @pl.when(j > 1)
             def _():
-                send_chunk(l, j - 1, 0 if h == 2 else h)
+                for what in ((B_Q, B_KV) if h == 1 else (A_ALL,)):
+                    send_chunk(l, j - 1, what)
             return 0
 
         lax.fori_loop(0, nchip, body, 0)
-        send_sibling(l, 0 if h == 2 else h)
+        for what in ((B_Q, B_KV) if h == 1 else (A_ALL,)):
+            send_sibling(l, what)
         for half in ((0, 1) if h == 2 else (h,)):
             keep_own(l, half)
 
@@ -284,24 +283,26 @@
 
         lax.fori_loop(0, nblk, body, 0)
 
-    def bulk(l, t, ssem, rsem):
-        r = qkv.at[l, t, pl.ds(0, others), :]
+    def bulk(l, ts, n, ssem, rsem):
+        r = qkv.at[l, ts, pl.ds(0, n * seg), :]
         return remote(r, r, ssem, rsem, me)
 
-    def recv(l, half, ts):
-        for t in ts:
-            bulk(l, t, send_sem.at[l, half, t], recv_sem.at[l, half, t]).wait_recv()
+    def recv(l, what):
+        bulk(l, what[1], ncp - 1, send_sem.at[l, what[2]], recv_sem.at[l, what[2]]).wait_recv()
 
     def sent(l, half):
-        for t in range(3):
-            bulk(l, t, send_sem.at[l, half, t], recv_sem.at[l, half, t]).wait_send()
-        forward_sent(l, half)
+        for _, ts, sem in ((A_ALL,) if half == 0 else (B_Q, B_KV)):
+            bulk(l, ts, ncp - 1 - CORES, send_sem.at[l, sem], recv_sem.at[l, sem]).wait_send()
+        for hh in range(CORES):
+            far_copy(l, half, hh).wait_send()
+            for c in forward_copies(l, half, hh):
+                c.wait_send()
 
     def o_recv(l, half):
-        bulk(l, 0, osend_sem.at[l, half], orecv_sem.at[l, half]).wait_recv()
+        bulk(l, slice(0, 1), ncp - 1, osend_sem.at[l, half], orecv_sem.at[l, half]).wait_recv()
 
     def o_sent(l, half):
-        bulk(l, 0, osend_sem.at[l, half], orecv_sem.at[l, half]).wait_send()
+        bulk(l, slice(0, 1), ncp - 1, osend_sem.at[l, half], orecv_sem.at[l, half]).wait_send()
 
     def mlp_step(a, w13, w2c):
         g = jnp.dot(a, w13[0], preferred_element_type=F32)
@@ -356,24 +357,23 @@
 
     norm(g1_ref, 0, 2)
     project(0)
-    send_rest(0, 1, (2,))
+    send_far(0, 1)
+    send_rest(0, B_Q)
     start(wo_copies(0))
     start(tail_copies(0))
     for f in range(SLOTS):
         start(mlp_copies(0, f, f))
     forward(0, 0)
-    forward(0, 1)
     outs = []
     for l in range(n_layers):
         if l > 0:
             o_sent(l - 1, 0)
-        recv(l, 0, (0, 1, 2))
+        recv(l, A_ALL)
         attend_a(l)
         if l == 0:
-            send_rest(l, 1, (0, 1))
-        else:
-            forward(l, 1)
-        recv(l, 1, (2,))
+            send_rest(l, B_KV)
+        forward(l, 1)
+        recv(l, B_Q)
         attend_ba(l)
         more = l + 1 < n_layers
         if more:
@@ -382,7 +382,7 @@
             norm(g1_ref, l + 1, 0)
         if l > 0:
             o_sent(l - 1, 1)
-        recv(l, 1, (0, 1))
+        recv(l, B_KV)
         for i, c in enumerate((kc_ref, vc_ref)):
             cp = pltpu.make_async_copy(qkv.at[l, i], c.at[l], out_sem.at[l, i])
             cp.start()
@@ -464,7 +464,7 @@
             scratch_shapes=[
                 pltpu.VMEM((rows, dim), BF16),
                 pltpu.VMEM((rows, dim), BF16),
-                pltpu.VMEM((nchip, 3, CORES, rows, HEAD), BF16),
+                pltpu.VMEM((nchip, CORES, 3, rows, HEAD), BF16),
                 pltpu.VMEM((n_layers, 3, seq, HEAD), BF16),
                 pltpu.VMEM((n_layers, rows, ncp * HEAD), BF16),
                 pltpu.VMEM((seq, HEAD), BF16),
@@ -472,19 +472,20 @@
                 pltpu.VMEM((nb, QB, 128), F32),
                 pltpu.VMEM((nb, QB, HEAD), F32),
                 pltpu.VMEM((rows, dim), F32),
-                pltpu.VMEM((n_layers, 2, 3, CORES, rows // 2, HEAD), BF16),
+                pltpu.VMEM((n_layers, 2, CORES, 3, rows // 2, HEAD), BF16),
                 pltpu.VMEM((2, 3, dim, CORES * HEAD), BF16),
                 pltpu.VMEM((ncp * HEAD, dim), BF16),
                 pltpu.VMEM((SLOTS, 2, dim, FB), BF16),
                 pltpu.VMEM((SLOTS, FB, dim), BF16),
                 pltpu.VMEM((2, dim, tail), BF16),
                 pltpu.VMEM((tail, dim), BF16),
-                pltpu.SemaphoreType.DMA((n_layers, 2, 3)),
-                pltpu.SemaphoreType.DMA((n_layers, 2, 3)),
+                pltpu.SemaphoreType.DMA((n_layers, 3)),
+                pltpu.SemaphoreType.DMA((n_layers, 3)),
                 pltpu.SemaphoreType.DMA((n_layers, 2)),
                 pltpu.SemaphoreType.DMA((n_layers, 2)),
-                pltpu.SemaphoreType.DMA((n_layers, 2)),
-                pltpu.SemaphoreType.DMA((n_layers, 2)),
+                pltpu.SemaphoreType.DMA((n_layers, 2, CORES)),
+                pltpu.SemaphoreType.DMA((n_layers, 2, CORES)),
+                pltpu.SemaphoreType.DMA((n_layers, 2, CORES, 2)),
                 pltpu.SemaphoreType.DMA((2,)),
                 pltpu.SemaphoreType.DMA,
                 pltpu.SemaphoreType.DMA((SLOTS,)),

time: 269 us -> 279 us (1.037)
  Pallas kernels: 266 us -> 274 us
    pallas_call x1, Pallas kernels: 261 us -> 269 us  [body(): pl.pallas_call(functools.partial(_kernel, ncp), out_shape=(jax.ShapeDtype...]
where the time goes in v3:
time: 279 us; the launch traced here: 276 us
  Pallas kernels  274 us (98%)
    pallas_call x1, Pallas kernels, body(): pl.pallas_call(functools.partial(_kernel, ncp), out_shape=(jax.ShapeDtype...  269 us

profile of v3, /device:TPU:21, one launch (start us, length us, event | category | flops | bytes accessed | tf_op | source)
XLA Modules:
  0.0 276.5 jit_solution(14668509353588516410)
XLA Ops:
  0.6 0.7 convert_element_type.3
  1.3 0.5 fusion
  1.9 0.8 pad_maximum_fusion
  2.7 268.9 %shard_map.130 = (bf16[256,2048]{1,0:T(8,128)(2,1)}, bf16[2,4096,128]{2,1,0:T(8,128)(2,1)}, bf16[2,4096,128]{2,1,0:T(8,128)(2,1)}) custom-call(bf16[256,2048]{1,0:T(8,128)(2,1)} %x_ref.1, f32[256,128]{1,0:T(8,128)} %get-tuple-element.21.cos_ref, f32[256,128]{1,0:T(8,128)} %get-tuple-element.22.sin_ref, bf16[2,2048]{1,0:T(2,128)(2,1)} %g1_ref.1, ...), custom_call_target="tpu_custom_call" | custom-call | tf_op jit(solution)/shard_map/pallas_call | solution.py:457
  271.6 4.7 %shard_map.131 = (bf16[2,128,2048]{2,1,0:T(8,128)(2,1)}, bf16[2,4096,128]{2,1,0:T(8,128)(2,1)}, bf16[2,4096,128]{2,1,0:T(8,128)(2,1)}) custom-call(bf16[2,128,2048]{2,1,0:T(8,128)(2,1)} %bitcast.8, bf16[2,4096,128]{2,1,0:T(8,128)(2,1)} %get-tuple-element.10.refs_1_, bf16[2,4096,128]{2,1,0:T(8,128)(2,1)} %get-tuple-element.11.refs_2_), custom_call_target="tpu_custom_call" | custom-call | tf_op jit(solution)/shard_map/pallas_call | solution.py:432
  (1 shorter events, 0.0 us)

commit v4 on v3

--- a/solution.py
+++ b/solution.py
@@ -29,9 +29,9 @@
 
 def _kernel(ncp, x_ref, cos_ref, sin_ref, g1_ref, g2_ref, wq, wk, wv, wo, w1, w3, w2,
             y_ref, kc_ref, vc_ref,
-            x_s, h_s, stage, qkv, o_s, o_stage, m_s, l_s, acc_s, y_acc, relay,
+            x_s, h_s, stage, qkv, o_s, o_stage, m_s, l_s, acc_s, y_acc,
             wqkv_s, wo_s, w13_s, w2_s, w13t_s, w2t_s,
-            send_sem, recv_sem, osend_sem, orecv_sem, rsend_sem, rrecv_sem, fsend_sem,
+            send_sem, recv_sem, osend_sem, orecv_sem,
             wqkv_sem, wo_sem, wm_sem, wt_sem, out_sem):
     n_layers = wq.shape[0]
     rows, dim = x_ref.shape
@@ -127,29 +127,6 @@
         return remote(stage.at[j, hh, ts, pl.ds(half * seg, seg), :], qkv.at[l, ts, row_of(me, half), :],
                       send_sem.at[l, sem], recv_sem.at[l, sem], dev)
 
-    def hops(hh, sign):
-        step = (nchip // 4) if (hh == 0) == (sign > 0) else nchip - nchip // 4
-        return lax.rem(chip + step, nchip)
-
-    def far_copy(l, half, hh):
-        return remote(stage.at[0, hh, :, pl.ds(half * seg, seg), :], relay.at[l, half, hh],
-                      rsend_sem.at[l, half, hh], rrecv_sem.at[l, half, hh], hops(hh, 1) * CORES + core)
-
-    def send_far(l, half):
-        for hh in range(CORES):
-            far_copy(l, half, hh).start()
-
-    def forward_copies(l, half, hh):
-        src = hops(hh, -1) * CORES + core
-        return [remote(relay.at[l, half, hh, ts], qkv.at[l, ts, row_of(src, half), :],
-                       fsend_sem.at[l, half, hh, i], recv_sem.at[l, sem], hops(hh, 1) * CORES + hh)
-                for i, (_, ts, sem) in enumerate((A_ALL,) if half == 0 else (B_Q, B_KV))]
-
-    def forward(l, half):
-        for hh in range(CORES):
-            far_copy(l, half, hh).wait_recv()
-            start(forward_copies(l, half, hh))
-
     def send_chunk(l, j, what):
         for hh in range(CORES):
             piece(l, j, hh, what).start()
@@ -157,8 +134,8 @@
     def send_sibling(l, what):
         piece(l, last, 1 - core, what).start()
 
-    def send_rest(l, what):
-        lax.fori_loop(1, last, lambda j, _: (send_chunk(l, j, what), 0)[1], 0)
+    def send_all(l, what):
+        lax.fori_loop(0, last, lambda j, _: (send_chunk(l, j, what), 0)[1], 0)
         send_sibling(l, what)
 
     def keep_own(l, half):
@@ -190,21 +167,20 @@
                 def _():
                     start(wqkv_copies(p + 1, j + 2 - nchip))
 
-            @pl.when(j == 1)
+            if p == 0:
+                @pl.when(j == 1)
+                def _():
+                    pl.semaphore_wait(barrier, ncp - 1)
+
+            @pl.when(j > 0)
             def _():
-                if p == 0:
-                    pl.semaphore_wait(barrier, ncp - 1)
-                send_far(l, 0 if h == 2 else h)
-
-            @pl.when(j > 1)
-            def _():
-                for what in ((B_Q, B_KV) if h == 1 else (A_ALL,)):
-                    send_chunk(l, j - 1, what)
+                send_chunk(l, j - 1, B_Q if h == 1 else A_ALL)
             return 0
 
         lax.fori_loop(0, nchip, body, 0)
-        for what in ((B_Q, B_KV) if h == 1 else (A_ALL,)):
-            send_sibling(l, what)
+        send_sibling(l, B_Q if h == 1 else A_ALL)
+        if h == 1:
+            send_all(l, B_KV)
         for half in ((0, 1) if h == 2 else (h,)):
             keep_own(l, half)
 
@@ -292,11 +268,7 @@
 
     def sent(l, half):
         for _, ts, sem in ((A_ALL,) if half == 0 else (B_Q, B_KV)):
-            bulk(l, ts, ncp - 1 - CORES, send_sem.at[l, sem], recv_sem.at[l, sem]).wait_send()
-        for hh in range(CORES):
-            far_copy(l, half, hh).wait_send()
-            for c in forward_copies(l, half, hh):
-                c.wait_send()
+            bulk(l, ts, ncp - 1, send_sem.at[l, sem], recv_sem.at[l, sem]).wait_send()
 
     def o_recv(l, half):
         bulk(l, slice(0, 1), ncp - 1, osend_sem.at[l, half], orecv_sem.at[l, half]).wait_recv()
@@ -310,7 +282,7 @@
         u = (g * (1.0 / (1.0 + jnp.exp(-g))) * u).astype(BF16)
         return jnp.dot(u, w2c, preferred_element_type=F32)
 
-    def dense(p, midway=None):
+    def dense(p):
         l, h = mpasses[p]
         sl = part[h]
         reload = p + 1 < len(mpasses) and mpasses[p + 1][0] != l
@@ -348,8 +320,6 @@
                 def _():
                     start(mlp_copies(p + 1, f + SLOTS - nf, slot))
 
-            if midway is not None:
-                pl.when(f == nf // 2)(midway)
             return 0
 
         lax.fori_loop(0, nf, body, 0)
@@ -357,13 +327,11 @@
 
     norm(g1_ref, 0, 2)
     project(0)
-    send_far(0, 1)
-    send_rest(0, B_Q)
+    send_all(0, B_Q)
     start(wo_copies(0))
     start(tail_copies(0))
     for f in range(SLOTS):
         start(mlp_copies(0, f, f))
-    forward(0, 0)
     outs = []
     for l in range(n_layers):
         if l > 0:
@@ -371,8 +339,7 @@
         recv(l, A_ALL)
         attend_a(l)
         if l == 0:
-            send_rest(l, B_KV)
-        forward(l, 1)
+            send_all(l, B_KV)
         recv(l, B_Q)
         attend_ba(l)
         more = l + 1 < n_layers
@@ -392,7 +359,7 @@
         if more:
             project(2 * l + 1)
             o_recv(l, 1)
-            dense(2 * l + 1, midway=lambda: forward(l + 1, 0))
+            dense(2 * l + 1)
             norm(g1_ref, l + 1, 1)
             sent(l, 1)
             project(2 * l + 2)
@@ -472,7 +439,6 @@
                 pltpu.VMEM((nb, QB, 128), F32),
                 pltpu.VMEM((nb, QB, HEAD), F32),
                 pltpu.VMEM((rows, dim), F32),
-                pltpu.VMEM((n_layers, 2, CORES, 3, rows // 2, HEAD), BF16),
                 pltpu.VMEM((2, 3, dim, CORES * HEAD), BF16),
                 pltpu.VMEM((ncp * HEAD, dim), BF16),
                 pltpu.VMEM((SLOTS, 2, dim, FB), BF16),
@@ -483,9 +449,6 @@
                 pltpu.SemaphoreType.DMA((n_layers, 3)),
                 pltpu.SemaphoreType.DMA((n_layers, 2)),
                 pltpu.SemaphoreType.DMA((n_layers, 2)),
-                pltpu.SemaphoreType.DMA((n_layers, 2, CORES)),
-                pltpu.SemaphoreType.DMA((n_layers, 2, CORES)),
-                pltpu.SemaphoreType.DMA((n_layers, 2, CORES, 2)),
                 pltpu.SemaphoreType.DMA((2,)),
                 pltpu.SemaphoreType.DMA,
                 pltpu.SemaphoreType.DMA((SLOTS,)),

time: 279 us -> 239 us (0.86)
  Pallas kernels: 274 us -> 235 us
    pallas_call x1, Pallas kernels: 269 us -> 231 us  [body(): pl.pallas_call(functools.partial(_kernel, ncp), out_shape=(jax.ShapeDtype...]
where the time goes in v4:
time: 239 us; the launch traced here: 238 us
  Pallas kernels  235 us (98%)
    pallas_call x1, Pallas kernels, body(): pl.pallas_call(functools.partial(_kernel, ncp), out_shape=(jax.ShapeDtype...  231 us

profile of v4, /device:TPU:21, one launch (start us, length us, event | category | flops | bytes accessed | tf_op | source)
XLA Modules:
  0.0 238.3 jit_solution(6120686105740228463)
XLA Ops:
  0.6 0.7 convert_element_type.3
  1.3 0.5 fusion
  1.9 0.8 pad_maximum_fusion
  2.7 230.7 %shard_map.130 = (bf16[256,2048]{1,0:T(8,128)(2,1)}, bf16[2,4096,128]{2,1,0:T(8,128)(2,1)}, bf16[2,4096,128]{2,1,0:T(8,128)(2,1)}) custom-call(bf16[256,2048]{1,0:T(8,128)(2,1)} %x_ref.1, f32[256,128]{1,0:T(8,128)} %get-tuple-element.21.cos_ref, f32[256,128]{1,0:T(8,128)} %get-tuple-element.22.sin_ref, bf16[2,2048]{1,0:T(2,128)(2,1)} %g1_ref.1, ...), custom_call_target="tpu_custom_call" | custom-call | tf_op jit(solution)/shard_map/pallas_call | solution.py:424
  233.4 4.7 %shard_map.131 = (bf16[2,128,2048]{2,1,0:T(8,128)(2,1)}, bf16[2,4096,128]{2,1,0:T(8,128)(2,1)}, bf16[2,4096,128]{2,1,0:T(8,128)(2,1)}) custom-call(bf16[2,128,2048]{2,1,0:T(8,128)(2,1)} %bitcast.8, bf16[2,4096,128]{2,1,0:T(8,128)(2,1)} %get-tuple-element.10.refs_1_, bf16[2,4096,128]{2,1,0:T(8,128)(2,1)} %get-tuple-element.11.refs_2_), custom_call_target="tpu_custom_call" | custom-call | tf_op jit(solution)/shard_map/pallas_call | solution.py:399
  (1 shorter events, 0.0 us)

commit v5 on v4

--- a/solution.py
+++ b/solution.py
@@ -23,8 +23,7 @@
     half = HEAD // 2
     inv = 1.0 / (10000.0 ** (jnp.arange(half, dtype=F32) * (2.0 / HEAD)))
     ang = pos.astype(F32)[:, None] * inv
-    c, sn = jnp.cos(ang), jnp.sin(ang)
-    return jnp.concatenate([c, c], axis=-1), jnp.concatenate([-sn, sn], axis=-1)
+    return jnp.cos(ang), jnp.sin(ang)
 
 
 def _kernel(ncp, x_ref, cos_ref, sin_ref, g1_ref, g2_ref, wq, wk, wv, wo, w1, w3, w2,
@@ -104,6 +103,8 @@
 
         lax.fori_loop(first, part[h].stop // blk, body, 0)
 
+    x_in = pltpu.make_async_copy(x_ref, x_s, out_sem.at[0, 0])
+    x_in.start()
     start(wqkv_copies(0, 0))
     start(wqkv_copies(0, 1))
     barrier = pltpu.get_barrier_semaphore()
@@ -113,7 +114,7 @@
         return 0
 
     lax.fori_loop(0, ncp - 1, sig, 0)
-    x_s[...] = x_ref[...]
+    x_in.wait()
 
     def row_of(dev, half):
         r = dev * seg if half == 0 else (nseg - 1 - dev) * seg
@@ -144,7 +145,8 @@
     def project(p):
         l, h = qpasses[p]
         sl = part[h]
-        cosv, sinv = cos_ref[sl, :], sin_ref[sl, :]
+        c, sn = cos_ref[sl, :], sin_ref[sl, :]
+        cosv, sinv = jnp.concatenate([c, c], axis=1), jnp.concatenate([-sn, sn], axis=1)
 
         def body(j, _):
             slot = lax.rem(p * nchip + j, 2)
@@ -338,13 +340,13 @@
             o_sent(l - 1, 0)
         recv(l, A_ALL)
         attend_a(l)
-        if l == 0:
-            send_all(l, B_KV)
         recv(l, B_Q)
         attend_ba(l)
         more = l + 1 < n_layers
         if more:
             o_recv(l, 0)
+            if l == 0:
+                send_all(l, B_KV)
             dense(2 * l)
             norm(g1_ref, l + 1, 0)
         if l > 0:
@@ -426,7 +428,7 @@
             out_shape=(jax.ShapeDtypeStruct((rows, dim), BF16),
                        jax.ShapeDtypeStruct((n_layers, seq, HEAD), BF16),
                        jax.ShapeDtypeStruct((n_layers, seq, HEAD), BF16)),
-            in_specs=[vm] * 5 + [hbm] * 7,
+            in_specs=[hbm] + [vm] * 4 + [hbm] * 7,
             out_specs=(hbm,) * 3,
             scratch_shapes=[
                 pltpu.VMEM((rows, dim), BF16),

time: 239 us -> 243 us (1.017)
  Pallas kernels: 235 us -> 238 us
    pallas_call x1, Pallas kernels: 231 us -> 233 us  [body(): pl.pallas_call(functools.partial(_kernel, ncp), out_shape=(jax.ShapeDtype...]
where the time goes in v5:
time: 243 us; the launch traced here: 241 us
  Pallas kernels  238 us (98%)
    pallas_call x1, Pallas kernels, body(): pl.pallas_call(functools.partial(_kernel, ncp), out_shape=(jax.ShapeDtype...  233 us

profile of v5, /device:TPU:21, one launch (start us, length us, event | category | flops | bytes accessed | tf_op | source)
XLA Modules:
  0.0 240.6 jit_solution(5523272041530809068)
XLA Ops:
  0.6 0.7 convert_element_type.3
  1.3 1.2 multiply_sine_fusion
  2.6 233.2 %shard_map.130 = (bf16[256,2048]{1,0:T(8,128)(2,1)}, bf16[2,4096,128]{2,1,0:T(8,128)(2,1)}, bf16[2,4096,128]{2,1,0:T(8,128)(2,1)}) custom-call(bf16[256,2048]{1,0:T(8,128)(2,1)} %x_ref.1, f32[256,64]{1,0:T(8,128)} %get-tuple-element.19.cos_ref, f32[256,64]{1,0:T(8,128)} %get-tuple-element.18.sin_ref, bf16[2,2048]{1,0:T(2,128)(2,1)} %g1_ref.1, ...), custom_call_target="tpu_custom_call" | custom-call | tf_op jit(solution)/shard_map/pallas_call | solution.py:426
  235.7 4.7 %shard_map.131 = (bf16[2,128,2048]{2,1,0:T(8,128)(2,1)}, bf16[2,4096,128]{2,1,0:T(8,128)(2,1)}, bf16[2,4096,128]{2,1,0:T(8,128)(2,1)}) custom-call(bf16[2,128,2048]{2,1,0:T(8,128)(2,1)} %bitcast.8, bf16[2,4096,128]{2,1,0:T(8,128)(2,1)} %get-tuple-element.10.refs_1_, bf16[2,4096,128]{2,1,0:T(8,128)(2,1)} %get-tuple-element.11.refs_2_), custom_call_target="tpu_custom_call" | custom-call | tf_op jit(solution)/shard_map/pallas_call | solution.py:401
  (1 shorter events, 0.0 us)
